TPU v7x, 32 devices: a whole 2x2x4 slice. The times are simulated.
32 devices in a mesh: chan: 4 (over x, core), az: 8 (over z, y).
Axes of the slice: x: 2, y: 2, z: 4, core: 2. Of those that a mesh axis runs over, the one named last changes fastest.
Arguments:
- signal: bfloat16 [4, 2, 128, 8192], P('chan', None, 'az'), may hold values from -6 to 6
- tap_table: float32 [64, 16], replicated, may hold values from -1.5 to 1.5
- range_shift: int32 [1024], P('az'), may hold values from -8 to 8
- tap_index: int32 [1024], P('az'), may hold values from 0 to 63
- ref_channel: int32 [8], P('az'), may hold values from 0 to 3
Outputs:
- picture: float32 [4, 2, 128, 1024], P('chan', None, None, 'az')
All inputs are finite; a program needn't handle non-finite values.
Results may differ from a plain program's by a relative error of at most 0.012.
Values may be sent and summed in bfloat16 or wider, within the bound.
A program may use at most 64 MiB of HBM per device.

v0:
```python
import math
import jax
import jax.numpy as jnp
from jax import lax
from jax.sharding import PartitionSpec as P

RF1 = 64
RF2 = 128
TAPS = 16
NTAB = 64
GUARD = 16
HALO = 16
PRECISE = lax.Precision.HIGH


def dft_table(length, orient):
    counter = jnp.arange(length, dtype=jnp.int32)
    phase = counter[:, None] * counter[None, :] % length
    angle = 2.0 * math.pi / length * phase.astype(jnp.float32)
    return (jnp.cos(angle), orient * jnp.sin(angle))


def twiddle_table(lead_size, tail_size, orient):
    lead_idx = jnp.arange(lead_size, dtype=jnp.int32)
    tail_idx = jnp.arange(tail_size, dtype=jnp.int32)
    phase = lead_idx[:, None] * tail_idx[None, :] % (lead_size * tail_size)
    angle = 2.0 * math.pi / (lead_size * tail_size) * phase.astype(jnp.float32)
    return (jnp.cos(angle), orient * jnp.sin(angle))


def split_table(table):
    upper = table.astype(jnp.bfloat16)
    lower = (table - upper.astype(jnp.float32)).astype(jnp.bfloat16)
    return (upper, lower)


def lead_product(table, data):
    if data.dtype == jnp.bfloat16:
        upper, lower = split_table(table)
        first = jnp.einsum("ka,rab->rkb", upper, data, preferred_element_type=jnp.float32)
        return first + jnp.einsum("ka,rab->rkb", lower, data, preferred_element_type=jnp.float32)
    return jnp.einsum("ka,rab->rkb", table, data, precision=PRECISE)


def along_last(real_part, imag_part, lead_size, tail_size, orient, factor):
    height = real_part.shape[0]
    real_in = real_part.reshape(height, lead_size, tail_size)
    imag_in = imag_part.reshape(height, lead_size, tail_size)
    lead_cos, lead_sin = dft_table(lead_size, orient)
    step_real = lead_product(lead_cos, real_in) - lead_product(lead_sin, imag_in)
    step_imag = lead_product(lead_cos, imag_in) + lead_product(lead_sin, real_in)
    twist_cos, twist_sin = twiddle_table(lead_size, tail_size, orient)
    turned_real = step_real * twist_cos[None] - step_imag * twist_sin[None]
    turned_imag = step_real * twist_sin[None] + step_imag * twist_cos[None]
    tail_cos, tail_sin = dft_table(tail_size, orient)
    out_real = jnp.einsum("rkb,bm->rmk", turned_real, tail_cos, precision=PRECISE) - jnp.einsum(
        "rkb,bm->rmk", turned_imag, tail_sin, precision=PRECISE
    )
    out_imag = jnp.einsum("rkb,bm->rmk", turned_real, tail_sin, precision=PRECISE) + jnp.einsum(
        "rkb,bm->rmk", turned_imag, tail_cos, precision=PRECISE
    )
    return (factor * out_real.reshape(height, -1), factor * out_imag.reshape(height, -1))


def along_first(real_part, imag_part, lead_size, tail_size, orient, factor):
    columns = real_part.shape[1]
    real_in = real_part.reshape(lead_size, tail_size, columns)
    imag_in = imag_part.reshape(lead_size, tail_size, columns)
    lead_cos, lead_sin = dft_table(lead_size, orient)
    step_real = jnp.einsum("ka,abs->kbs", lead_cos, real_in, precision=PRECISE) - jnp.einsum(
        "ka,abs->kbs", lead_sin, imag_in, precision=PRECISE
    )
    step_imag = jnp.einsum("ka,abs->kbs", lead_cos, imag_in, precision=PRECISE) + jnp.einsum(
        "ka,abs->kbs", lead_sin, real_in, precision=PRECISE
    )
    twist_cos, twist_sin = twiddle_table(lead_size, tail_size, orient)
    turned_real = step_real * twist_cos[:, :, None] - step_imag * twist_sin[:, :, None]
    turned_imag = step_real * twist_sin[:, :, None] + step_imag * twist_cos[:, :, None]
    tail_cos, tail_sin = dft_table(tail_size, orient)
    out_real = jnp.einsum("kbs,bm->mks", turned_real, tail_cos, precision=PRECISE) - jnp.einsum(
        "kbs,bm->mks", turned_imag, tail_sin, precision=PRECISE
    )
    out_imag = jnp.einsum("kbs,bm->mks", turned_real, tail_sin, precision=PRECISE) + jnp.einsum(
        "kbs,bm->mks", turned_imag, tail_cos, precision=PRECISE
    )
    return (factor * out_real.reshape(-1, columns), factor * out_imag.reshape(-1, columns))


def whiten(spec_real, spec_imag):
    inverse = lax.rsqrt(jnp.maximum(spec_real * spec_real + spec_imag * spec_imag, 1.0))
    return ((spec_real * inverse).astype(jnp.bfloat16), (-spec_imag * inverse).astype(jnp.bfloat16))


def band_product(frame, band_upper, band_lower):
    first = jnp.dot(frame, band_upper, preferred_element_type=jnp.float32)
    return first + jnp.dot(frame, band_lower, preferred_element_type=jnp.float32)


def shards(signal, tap_table, range_shift, tap_index, ref_channel):
    source_id = ref_channel[0]
    is_source = lax.axis_index("chan") == source_id
    own_data = signal[0]
    pul_dev = own_data.shape[1]
    samples_len = own_data.shape[2]
    slab_len = range_shift.shape[0]
    az_count = lax.axis_size("az")
    lag_count = slab_len * az_count
    factor_range = 1.0 / math.sqrt(samples_len)
    spec_real, spec_imag = along_last(own_data[0], own_data[1], RF1, RF2, -1.0, factor_range)
    masked_data = jnp.where(is_source, own_data, jnp.zeros_like(own_data))
    ref_data = lax.psum(masked_data, "chan").astype(jnp.float32).astype(jnp.bfloat16)
    ref_real, ref_imag = along_last(ref_data[0], ref_data[1], RF1, RF2, -1.0, factor_range)
    filter_low_real, filter_low_imag = whiten(ref_real, ref_imag)
    filter_real = filter_low_real.astype(jnp.float32)
    filter_imag = filter_low_imag.astype(jnp.float32)
    prod_real = spec_real * filter_real - spec_imag * filter_imag
    prod_imag = spec_real * filter_imag + spec_imag * filter_real
    lag_real, lag_imag = along_last(prod_real, prod_imag, RF1, RF2, 1.0, factor_range)
    compressed = jnp.stack(
        [lag_real[:, GUARD : GUARD + lag_count], lag_imag[:, GUARD : GUARD + lag_count]]
    ).astype(jnp.bfloat16)
    padded = jnp.pad(compressed, ((0, 0), (0, 0), (HALO, slab_len + HALO)))
    main_part = padded[:, :, :lag_count].reshape(2, pul_dev, az_count, slab_len)
    after_part = padded[:, :, slab_len : slab_len + lag_count].reshape(
        2, pul_dev, az_count, slab_len
    )[..., : 2 * HALO]
    widened = jnp.concatenate([main_part, after_part], axis=3).reshape(
        2, pul_dev, az_count * (slab_len + 2 * HALO)
    )
    framed = lax.all_to_all(widened, "az", split_axis=2, concat_axis=1, tiled=True)
    chooser = (tap_index[:, None] == jnp.arange(NTAB, dtype=jnp.int32)[None, :]).astype(jnp.float32)
    tap_rows = jnp.dot(chooser, tap_table, precision=lax.Precision.HIGHEST)
    source_pos = jnp.arange(slab_len + 2 * HALO, dtype=jnp.int32)[:, None, None]
    target_pos = (
        jnp.arange(slab_len, dtype=jnp.int32)[None, :, None]
        + HALO
        + range_shift[None, :, None]
        + jnp.arange(TAPS, dtype=jnp.int32)[None, None, :]
        - TAPS // 2
    )
    banded = jnp.sum(jnp.where(source_pos == target_pos, tap_rows[None], 0.0), axis=2)
    band_upper, band_lower = split_table(banded)
    aligned_real = band_product(framed[0], band_upper, band_lower)
    aligned_imag = band_product(framed[1], band_upper, band_lower)
    pulse_total = aligned_real.shape[0]
    doppler_real, doppler_imag = along_first(
        aligned_real, aligned_imag, az_count, pul_dev, -1.0, 1.0 / math.sqrt(pulse_total)
    )
    return jnp.stack([doppler_real, doppler_imag])[None]


def solution(mesh):
    return jax.shard_map(
        shards,
        mesh=mesh,
        in_specs=(P("chan", None, "az", None), P(), P("az"), P("az"), P("az")),
        out_specs=P("chan", None, None, "az"),
        check_vma=False,
    )
```

profile of v0, /device:TPU:0, one launch (start us, length us, event | category | flops | bytes accessed | tf_op | source)
XLA Modules:
  0.0 95.3 jit_solution(10513515113329657731)
XLA Ops:
  7.3 0.8 select_bitcast_fusion
  11.7 0.6 fusion.27
  12.4 0.6 fusion.10
  13.1 0.6 fusion.5
  15.6 30.3 %all-reduce.3.cloned.1.call-done = bf16[2,16,8192]{2,1,0:T(8,128)(2,1)} async-done(((bf16[2,16,8192]{2,1,0:T(8,128)(2,1)}), bf16[2,16,8192]{2,1,0:T(8,128)(2,1)}) %all-reduce.3.cloned.1.call-update) | async-done | bytes 524304 | tf_op jit(solution)/shard_map/psum | solution.py:111
  45.9 1.1 %slice_bitcast_fusion = (bf16[2,8,64,128]{3,1,2,0:T(8,128)(2,1)S(1)}, bf16[2,8,64,128]{3,1,2,0:T(8,128)(2,1)S(1)}) fusion(bf16[2,16,8192]{2,1,0:T(8,128)(2,1)} %all-reduce.3.cloned.1.call-done), kind=kLoop, calls=%fused_computation.71 | loop fusion | bytes 1048576
  50.3 1.4 %fusion.33 = f32[128,16,64]{0,2,1:T(8,128)} fusion(f32[16,64,128]{2,1,0:T(8,128)S(1)} %fusion.16, f32[16,64,128]{2,1,0:T(8,128)S(1)} %fusion.14, f32[64,128]{1,0:T(8,128)S(1)} %get-tuple-element.19, f32[64,128]{1,0:T(8,128)S(1)} %get-tuple-element.20), kind=kOutput, calls=%fused_computation.79 | convolution fusion | flops 101285888 | bytes 1638400 | tf_op jit(solution)/shard_map/rkb,bm->rmk/dot_general | solution.py:56
  51.7 1.6 %negate_bitcast_fusion = (f32[16,128,64]{1,2,0:T(8,128)}, f32[16,128,64]{1,2,0:T(8,128)}) fusion(f32[128,16,64]{0,2,1:T(8,128)S(1)} %fusion.32, f32[16,64,128]{2,1,0:T(8,128)S(1)} %fusion.16, f32[16,64,128]{2,1,0:T(8,128)S(1)} %fusion.14, f32[64,128]{1,0:T(8,128)S(1)} %get-tuple-element.19, f32[64,128]{1,0:T(8,128)S(1)} %get-tuple-element.20), kind=kOutput, calls=%fused_computation.62 | convolution fusion | flops 101810176 | bytes 2686976 | tf_op jit(solution)/shard_map/rkb,bm->rmk/dot_general | solution.py:59
  53.3 1.4 %copy.77 = f32[16,128,64]{2,1,0:T(8,128)S(1)} copy(f32[16,128,64]{1,2,0:T(8,128)} %get-tuple-element.8) | data formatting | bytes 1048576 | tf_op jit(solution)/shard_map/mul | solution.py:90
  54.7 1.0 %mul.962 = f32[16,64,128]{2,1,0:T(8,128)} reshape(f32[16,128,64]{2,1,0:T(8,128)S(1)} %copy.77) | data formatting | bytes 1048576 | tf_op jit(solution)/shard_map/mul | solution.py:90
  55.7 1.4 %copy.79 = f32[16,128,64]{2,1,0:T(8,128)S(1)} copy(f32[16,128,64]{1,2,0:T(8,128)} %get-tuple-element.7) | data formatting | bytes 1048576 | tf_op jit(solution)/shard_map/neg | solution.py:91
  57.1 1.0 %neg.13 = f32[16,64,128]{2,1,0:T(8,128)} reshape(f32[16,128,64]{2,1,0:T(8,128)S(1)} %copy.79) | data formatting | bytes 1048576 | tf_op jit(solution)/shard_map/neg | solution.py:91
  58.1 1.7 %fusion.8 = f32[16,128,64]{1,2,0:T(8,128)S(1)} fusion(f32[128,16,64]{0,2,1:T(8,128)} %fusion.33, f32[16,64,128]{2,1,0:T(8,128)S(1)} %fusion.16, f32[16,64,128]{2,1,0:T(8,128)S(1)} %fusion.14, f32[64,128]{1,0:T(8,128)S(1)} %get-tuple-element.19, f32[64,128]{1,0:T(8,128)S(1)} %get-tuple-element.20), kind=kOutput, calls=%fused_computation.25 | convolution fusion | flops 101564416 | bytes 2162688 | tf_op jit(solution)/shard_map/rkb,bm->rmk/dot_general | solution.py:56
  60.1 1.0 %mul.957 = f32[16,64,128]{2,1,0:T(8,128)} reshape(f32[16,128,64]{2,1,0:T(8,128)S(1)} %copy.76) | data formatting | bytes 1048576 | tf_op jit(solution)/shard_map/mul | solution.py:62
  61.5 1.2 %multiply_convert_fusion = (bf16[16,64,128]{2,1,0:T(8,128)(2,1)S(1)}, bf16[16,64,128]{2,1,0:T(8,128)(2,1)S(1)}) fusion(f32[16,64,128]{2,1,0:T(8,128)S(1)} %copy-done.3, f32[16,64,128]{2,1,0:T(8,128)S(1)} %copy-done.2, f32[16,64,128]{2,1,0:T(8,128)} %mul.957), kind=kLoop, calls=%fused_computation.61 | loop fusion | flops 917504 | bytes 2097152 | tf_op jit(solution)/shard_map/convert_element_type | solution.py:91
  62.7 0.7 fusion.84
  66.4 0.6 fusion.20
  67.9 0.6 fusion.19
  69.5 0.7 copy.82
  70.3 1.3 %reshape.214 = bf16[8,2,2560]{2,1,0:T(2,128)(2,1)} reshape(bf16[1280,2,16]{2,1,0:T(2,128)(2,1)S(1)} %bitcast.209) | data formatting | bytes 163840
  71.6 5.5 %all-to-all-start = ((bf16[8,2,2560]{2,1,0:T(2,128)(2,1)}), bf16[8,2,2560]{2,1,0:T(2,128)(2,1)S(1)}, u32[]{:S(2)}, u32[]{:S(2)}) async-start(bf16[8,2,2560]{2,1,0:T(2,128)(2,1)} %reshape.214), calls=%async_computation | async-start | bytes 163840 | tf_op jit(solution)/shard_map/all_to_all | solution.py:130
  77.5 6.7 %all-to-all-done = bf16[8,2,2560]{2,1,0:T(2,128)(2,1)S(1)} async-done(((bf16[8,2,2560]{2,1,0:T(2,128)(2,1)}), bf16[8,2,2560]{2,1,0:T(2,128)(2,1)S(1)}, u32[]{:S(2)}, u32[]{:S(2)}) %all-to-all-start) | async-done | bytes 81952 | tf_op jit(solution)/shard_map/all_to_all | solution.py:130
  84.6 0.6 copy.96
  87.8 0.7 maximum_bitcast_fusion
  (83 shorter events, 17.3 us)
Async XLA Ops:
  6.5 8.4 %copy-start = (f32[64,16]{0,1:T(8,128)S(1)}, f32[64,16]{0,1:T(8,128)}, u32[]{:S(2)}) copy-start(f32[64,16]{0,1:T(8,128)} %param.6) | copy-start | bytes 12292
  6.5 1.7 %copy-start.1 = (bf16[1,2,16,8192]{3,2,1,0:T(8,128)(2,1)S(1)}, bf16[1,2,16,8192]{3,2,1,0:T(8,128)(2,1)}, u32[]{:S(2)}) copy-start(bf16[1,2,16,8192]{3,2,1,0:T(8,128)(2,1)} %param.5) | copy-start | bytes 1572868
  6.5 39.3 %all-reduce.3.cloned.1.call-start = ((), (), s32[]{:S(2)}) async-start(), calls=%async_computation.1 | async-start | bytes 1048576 | tf_op jit(solution)/shard_map/psum | solution.py:111
  13.1 0.7 copy-start.4
  14.7 0.7 copy-start.5
  60.1 1.0 %copy-start.2 = (f32[16,64,128]{2,1,0:T(8,128)S(1)}, f32[16,64,128]{2,1,0:T(8,128)}, u32[]{:S(2)}) copy-start(f32[16,64,128]{2,1,0:T(8,128)} %mul.962) | copy-start | bytes 1572868
  60.1 1.4 %copy-start.3 = (f32[16,64,128]{2,1,0:T(8,128)S(1)}, f32[16,64,128]{2,1,0:T(8,128)}, u32[]{:S(2)}) copy-start(f32[16,64,128]{2,1,0:T(8,128)} %neg.13) | copy-start | bytes 1572868
  71.6 12.5 %all-to-all-start = ((bf16[8,2,2560]{2,1,0:T(2,128)(2,1)}), bf16[8,2,2560]{2,1,0:T(2,128)(2,1)S(1)}, u32[]{:S(2)}, u32[]{:S(2)}) async-start(bf16[8,2,2560]{2,1,0:T(2,128)(2,1)} %reshape.214), calls=%async_computation | async-start | bytes 163840 | tf_op jit(solution)/shard_map/all_to_all | solution.py:130
Sparse Core Ops, SparseCore 0:
  9.7 36.1 all-reduce.2
where the time goes:
time: 95.7 us; the launch traced here: 95.3 us
  waiting for transfers between devices  37 us (39%)
  matrix products  20.2 us (21%)
  between operations  14.7 us (15%)
  local copies, waits for them, and re-layouts  14.3 us (15%)
  starting transfers between devices  5.52 us (6%)
  other arithmetic  3.55 us (4%)
    psum x1, waiting for transfers between devices, shards(): lax.psum(masked_data, 'chan').astype(jnp.float32).astype(jnp.bfloat16)  30.3 us
    all_to_all x1, waiting for transfers between devices, shards(): lax.all_to_all(widened, 'az', split_axis=2, concat_axis=1, tiled=True)  6.7 us
    all_to_all x1, starting transfers between devices, shards(): lax.all_to_all(widened, 'az', split_axis=2, concat_axis=1, tiled=True)  5.52 us
    unnamed x22, local copies, waits for them, and re-layouts  3.93 us
    dot_general x3, matrix products, along_last(): jnp.einsum('rkb,bm->rmk', turned_imag, tail_sin, precision=PRECISE)  2.91 us
    dot_general x3, matrix products, along_last(): jnp.einsum('rkb,bm->rmk', turned_imag, tail_cos, precision=PRECISE)  2.87 us
    mul x6, local copies, waits for them, and re-layouts, along_last(): factor * out_real.reshape(height, -1)  2.63 us
    dot_general x3, matrix products, along_last(): jnp.einsum('rkb,bm->rmk', turned_real, tail_cos, precision=PRECISE)  2.63 us
  transfers between devices with their start and end apart: 2, of which 2 were waited for; matrix products, arithmetic and copies ran while one was open for 7% of the time, Pallas kernels for 0%

commit v1 on v0

--- a/solution.py
+++ b/solution.py
@@ -11,6 +11,11 @@
 GUARD = 16
 HALO = 16
 PRECISE = lax.Precision.HIGH
+
+
+def add_all(x, axis):
+    parts = lax.all_gather(x, axis)
+    return jnp.sum(parts, axis=0)
 
 
 def dft_table(length, orient):
@@ -108,7 +113,7 @@
     factor_range = 1.0 / math.sqrt(samples_len)
     spec_real, spec_imag = along_last(own_data[0], own_data[1], RF1, RF2, -1.0, factor_range)
     masked_data = jnp.where(is_source, own_data, jnp.zeros_like(own_data))
-    ref_data = lax.psum(masked_data, "chan").astype(jnp.float32).astype(jnp.bfloat16)
+    ref_data = add_all(masked_data, "chan").astype(jnp.float32).astype(jnp.bfloat16)
     ref_real, ref_imag = along_last(ref_data[0], ref_data[1], RF1, RF2, -1.0, factor_range)
     filter_low_real, filter_low_imag = whiten(ref_real, ref_imag)
     filter_real = filter_low_real.astype(jnp.float32)

time: 95.7 us -> 86.5 us (0.904)
  waiting for transfers between devices: 37 us -> 25.7 us
  other arithmetic: 3.55 us -> 5.7 us
    psum x1 -> x0, waiting for transfers between devices: 30.3 us -> none  [shards(): lax.psum(masked_data, 'chan').astype(jnp.float32).astype(jnp.bfloat16)]
    all_gather x0 -> x1, waiting for transfers between devices: none -> 19 us  [add_all(): parts = lax.all_gather(x, axis)]
    reduce_sum x0 -> x1, other arithmetic: none -> 1.98 us  [add_all(): return jnp.sum(parts, axis=0)]
    unnamed x22, local copies, waits for them, and re-layouts: 3.93 us -> 2.1 us
    mul x6, local copies, waits for them, and re-layouts: 2.63 us -> 3.78 us  [along_last(): factor * out_real.reshape(height, -1)]
  transfers between devices with their start and end apart: 2 -> 2, of which waited for: 2 -> 2; matrix products, arithmetic and copies ran while one was open for 7% -> 8% of each run, Pallas kernels for 0% -> 0%
where the time goes in v1:
time: 86.5 us; the launch traced here: 86.1 us
  waiting for transfers between devices  25.7 us (30%)
  matrix products  20.9 us (24%)
  between operations  14.7 us (17%)
  local copies, waits for them, and re-layouts  13.6 us (16%)
  other arithmetic  5.7 us (7%)
  starting transfers between devices  5.51 us (6%)
    all_gather x1, waiting for transfers between devices, add_all(): parts = lax.all_gather(x, axis)  19 us
    all_to_all x1, waiting for transfers between devices, shards(): lax.all_to_all(widened, 'az', split_axis=2, concat_axis=1, tiled=True)  6.7 us
    all_to_all x1, starting transfers between devices, shards(): lax.all_to_all(widened, 'az', split_axis=2, concat_axis=1, tiled=True)  5.51 us
    mul x6, local copies, waits for them, and re-layouts, along_last(): factor * out_real.reshape(height, -1)  3.78 us
    dot_general x3, matrix products, along_last(): jnp.einsum('rkb,bm->rmk', turned_imag, tail_sin, precision=PRECISE)  3.71 us
    dot_general x3, matrix products, along_last(): jnp.einsum('rkb,bm->rmk', turned_imag, tail_cos, precision=PRECISE)  2.83 us
    dot_general x3, matrix products, along_last(): jnp.einsum('rkb,bm->rmk', turned_real, tail_cos, precision=PRECISE)  2.64 us
    dot_general x8, matrix products, lead_product(): jnp.einsum('ka,rab->rkb', lower, data, preferred_element_type=jnp.float32)  2.6 us
  transfers between devices with their start and end apart: 2, of which 2 were waited for; matrix products, arithmetic and copies ran while one was open for 8% of the time, Pallas kernels for 0%

profile of v1, /device:TPU:0, one launch (start us, length us, event | category | flops | bytes accessed | tf_op | source)
XLA Modules:
  0.0 86.1 jit_solution(9606427613301117022)
XLA Ops:
  7.3 0.8 broadcast_select_fusion
  11.7 0.6 fusion.10
  12.9 0.6 fusion.27
  13.5 0.6 fusion.5
  15.2 19.0 %all-gather.2.cloned.1.call-done = bf16[4,2,16,8192]{3,2,1,0:T(8,128)(2,1)} async-done(((bf16[1,2,16,8192]{3,2,1,0:T(8,128)(2,1)}), bf16[4,2,16,8192]{3,2,1,0:T(8,128)(2,1)}) %all-gather.2.cloned.1.call-update) | async-done | bytes 2097168 | tf_op jit(solution)/shard_map/all_gather | solution.py:17
  34.2 2.0 %reduce_sum.21 = bf16[2,16,8192]{2,1,0:T(8,128)(2,1)S(1)} reduce(bf16[4,2,16,8192]{3,2,1,0:T(8,128)(2,1)} %all-gather.2.cloned.1.call-done, bf16[]{:T(256)} %constant.132.clone.1), dimensions={0}, to_apply=%region_0.1 | reduce | flops 786432 | bytes 2621442 | tf_op jit(solution)/shard_map/reduce_sum | solution.py:18
  39.6 1.4 %fusion.33 = f32[128,16,64]{0,2,1:T(8,128)} fusion(f32[16,64,128]{2,1,0:T(8,128)S(1)} %fusion.16, f32[16,64,128]{2,1,0:T(8,128)S(1)} %fusion.14, f32[64,128]{1,0:T(8,128)S(1)} %get-tuple-element.19, f32[64,128]{1,0:T(8,128)S(1)} %get-tuple-element.20), kind=kOutput, calls=%fused_computation.79 | convolution fusion | flops 101285888 | bytes 1638400 | tf_op jit(solution)/shard_map/rkb,bm->rmk/dot_general | solution.py:61
  41.0 1.6 %negate_bitcast_fusion = (f32[16,128,64]{1,2,0:T(8,128)}, f32[16,128,64]{1,2,0:T(8,128)}) fusion(f32[128,16,64]{0,2,1:T(8,128)S(1)} %fusion.32, f32[16,64,128]{2,1,0:T(8,128)S(1)} %fusion.16, f32[16,64,128]{2,1,0:T(8,128)S(1)} %fusion.14, f32[64,128]{1,0:T(8,128)S(1)} %get-tuple-element.19, f32[64,128]{1,0:T(8,128)S(1)} %get-tuple-element.20), kind=kOutput, calls=%fused_computation.62 | convolution fusion | flops 101810176 | bytes 2686976 | tf_op jit(solution)/shard_map/rkb,bm->rmk/dot_general | solution.py:64
  42.6 1.4 %copy.77 = f32[16,128,64]{2,1,0:T(8,128)S(1)} copy(f32[16,128,64]{1,2,0:T(8,128)} %get-tuple-element.8) | data formatting | bytes 1048576 | tf_op jit(solution)/shard_map/mul | solution.py:95
  44.0 1.0 %mul.962 = f32[16,64,128]{2,1,0:T(8,128)} reshape(f32[16,128,64]{2,1,0:T(8,128)S(1)} %copy.77) | data formatting | bytes 1048576 | tf_op jit(solution)/shard_map/mul | solution.py:95
  45.0 1.4 %copy.79 = f32[16,128,64]{2,1,0:T(8,128)S(1)} copy(f32[16,128,64]{1,2,0:T(8,128)} %get-tuple-element.7) | data formatting | bytes 1048576 | tf_op jit(solution)/shard_map/neg | solution.py:96
  46.4 1.0 %neg.13 = f32[16,64,128]{2,1,0:T(8,128)} reshape(f32[16,128,64]{2,1,0:T(8,128)S(1)} %copy.79) | data formatting | bytes 1048576 | tf_op jit(solution)/shard_map/neg | solution.py:96
  47.4 2.5 %fusion.8 = f32[16,128,64]{1,2,0:T(8,128)} fusion(f32[128,16,64]{0,2,1:T(8,128)} %fusion.33, f32[16,64,128]{2,1,0:T(8,128)S(1)} %fusion.16, f32[16,64,128]{2,1,0:T(8,128)S(1)} %fusion.14, f32[64,128]{1,0:T(8,128)S(1)} %get-tuple-element.19, f32[64,128]{1,0:T(8,128)S(1)} %get-tuple-element.20), kind=kOutput, calls=%fused_computation.25 | convolution fusion | flops 101564416 | bytes 2162688 | tf_op jit(solution)/shard_map/rkb,bm->rmk/dot_general | solution.py:61
  49.9 1.5 %copy.76 = f32[16,128,64]{2,1,0:T(8,128)S(1)} copy(f32[16,128,64]{1,2,0:T(8,128)} %fusion.8) | data formatting | bytes 1048576 | tf_op jit(solution)/shard_map/mul | solution.py:67
  51.3 1.0 %mul.957 = f32[16,64,128]{2,1,0:T(8,128)} reshape(f32[16,128,64]{2,1,0:T(8,128)S(1)} %copy.76) | data formatting | bytes 1048576 | tf_op jit(solution)/shard_map/mul | solution.py:67
  52.3 1.4 %multiply_convert_fusion = (bf16[16,64,128]{2,1,0:T(8,128)(2,1)S(1)}, bf16[16,64,128]{2,1,0:T(8,128)(2,1)S(1)}) fusion(f32[16,64,128]{2,1,0:T(8,128)S(1)} %copy-done.3, f32[16,64,128]{2,1,0:T(8,128)S(1)} %copy-done.2, f32[16,64,128]{2,1,0:T(8,128)} %mul.957), kind=kLoop, calls=%fused_computation.61 | loop fusion | flops 917504 | bytes 2097152 | tf_op jit(solution)/shard_map/convert_element_type | solution.py:96
  57.2 0.6 fusion.20
  58.7 0.6 fusion.19
  60.4 0.7 copy.82
  61.1 1.3 %reshape.211 = bf16[8,2,2560]{2,1,0:T(2,128)(2,1)} reshape(bf16[1280,2,16]{2,1,0:T(2,128)(2,1)S(1)} %bitcast.207) | data formatting | bytes 163840
  62.4 5.5 %all-to-all-start = ((bf16[8,2,2560]{2,1,0:T(2,128)(2,1)}), bf16[8,2,2560]{2,1,0:T(2,128)(2,1)S(1)}, u32[]{:S(2)}, u32[]{:S(2)}) async-start(bf16[8,2,2560]{2,1,0:T(2,128)(2,1)} %reshape.211), calls=%async_computation | async-start | bytes 163840 | tf_op jit(solution)/shard_map/all_to_all | solution.py:135
  68.3 6.7 %all-to-all-done = bf16[8,2,2560]{2,1,0:T(2,128)(2,1)S(1)} async-done(((bf16[8,2,2560]{2,1,0:T(2,128)(2,1)}), bf16[8,2,2560]{2,1,0:T(2,128)(2,1)S(1)}, u32[]{:S(2)}, u32[]{:S(2)}) %all-to-all-start) | async-done | bytes 81952 | tf_op jit(solution)/shard_map/all_to_all | solution.py:135
  75.4 0.6 copy.96
  78.6 0.7 maximum_bitcast_fusion
  (84 shorter events, 16.8 us)
Async XLA Ops:
  6.5 8.4 %copy-start = (f32[64,16]{0,1:T(8,128)S(1)}, f32[64,16]{0,1:T(8,128)}, u32[]{:S(2)}) copy-start(f32[64,16]{0,1:T(8,128)} %param.6) | copy-start | bytes 12292
  6.5 1.6 %copy-start.1 = (bf16[1,2,16,8192]{3,2,1,0:T(8,128)(2,1)S(1)}, bf16[1,2,16,8192]{3,2,1,0:T(8,128)(2,1)}, u32[]{:S(2)}) copy-start(bf16[1,2,16,8192]{3,2,1,0:T(8,128)(2,1)} %param.5) | copy-start | bytes 1572868
  6.5 27.7 %all-gather.2.cloned.1.call-start = ((), (), s32[]{:S(2)}) async-start(), calls=%async_computation.1 | async-start | bytes 2621440 | tf_op jit(solution)/shard_map/all_gather | solution.py:17
  14.1 0.8 copy-start.4
  14.1 0.8 copy-start.5
  49.9 2.5 %copy-start.2 = (f32[16,64,128]{2,1,0:T(8,128)S(1)}, f32[16,64,128]{2,1,0:T(8,128)}, u32[]{:S(2)}) copy-start(f32[16,64,128]{2,1,0:T(8,128)} %mul.962) | copy-start | bytes 1572868
  49.9 2.5 %copy-start.3 = (f32[16,64,128]{2,1,0:T(8,128)S(1)}, f32[16,64,128]{2,1,0:T(8,128)}, u32[]{:S(2)}) copy-start(f32[16,64,128]{2,1,0:T(8,128)} %neg.13) | copy-start | bytes 1572868
  62.4 12.5 %all-to-all-start = ((bf16[8,2,2560]{2,1,0:T(2,128)(2,1)}), bf16[8,2,2560]{2,1,0:T(2,128)(2,1)S(1)}, u32[]{:S(2)}, u32[]{:S(2)}) async-start(bf16[8,2,2560]{2,1,0:T(2,128)(2,1)} %reshape.211), calls=%async_computation | async-start | bytes 163840 | tf_op jit(solution)/shard_map/all_to_all | solution.py:135
Sparse Core Ops, SparseCore 0:
  8.9 25.2 all-gather.1
